TPU v7x, 256 devices: a 4x2x16 block of a 4x16x16 slice. The times are simulated.
256 devices in a mesh: groups: 2 (over y), heads: 32 (over z, core), batch: 4 (over x).
Axes of the slice: x: 4, y: 2, z: 16, core: 2. Of those that a mesh axis runs over, the one named last changes fastest.
The devices are a block of a 4x16x16 slice.
Arguments:
- queries: bfloat16 [128, 8192], P(('groups', 'batch'), 'heads'), parts along dimension 0, may hold values from -110 to 110
- new_kv: bfloat16 [64, 64, 256], P(('groups', 'heads'), 'batch'), parts along dimension 0, may hold values from -15 to 15
- kv_pool: bfloat16 [64, 192, 128, 256], P(('groups', 'heads'), 'batch'), parts along dimension 0, may hold values from -6 to 6
- page_counts: int32 [8, 16], P(('groups', 'batch')), parts along dimension 0, may hold values from 1 to 6, 48 in all within a row
- last_fill: int32 [8, 16], P(('groups', 'batch')), parts along dimension 0, may hold values from 1 to 128
- page_order: int32 [8, 48], P(('groups', 'batch')), parts along dimension 0, may hold values from 0 to 47, each once within a row
- hidden: bfloat16 [128, 8192], P(('groups', 'batch')), parts along dimension 0, may hold values from -0.59765625 to 0.59765625
- out_weight: bfloat16 [8192, 8192], P('heads'), may hold values from -0.5 to 0.5
- norm_gain: bfloat16 [8192], replicated, may hold values from 0.099609375 to 1.8984375
- sectioned: bfloat16 [64, 4, 8, 128, 256], P(('groups', 'heads'), 'batch'), parts along dimension 0, may hold values from -6 to 6
- routes: int32 [64, 4, 8, 1], P(('groups', 'heads'), 'batch'), parts along dimension 0, may hold values from 0 to 7; in each aligned block of 8 rows (0 to 7, 8 to 15, ..., all dimensions but the last counted through in order) at most 2 rows name the same one
Outputs:
- residual_out: bfloat16 [128, 8192], P(('groups', 'batch')), parts along dimension 0
- normed: bfloat16 [128, 8192], P(('groups', 'batch')), parts along dimension 0
- arrival: bfloat16 [64, 4, 32, 2, 128, 256], P(('groups', 'heads'), 'batch'), parts along dimension 0
There are 2 independent parts, one for each index of `groups`. A program takes and returns all parts, laid end to end along the dimension named above; an argument that names none is the same for every part. Nothing has to cross between parts.
Inputs may be any that keep to these rules, and one draw needn't show every extreme that they name: `routes`: every key-value head is named by at most 2 sectioned pages of one device. `page_counts`: the page counts of one batch owner sum to 48.
All inputs are finite; a program needn't handle non-finite values.
Results may differ from a plain program's by a relative error of at most 0.0066.
Values may be sent and summed in bfloat16 or wider, within the bound.
A program may use at most 64 MiB of HBM per device.

v0:
```python
import jax
import jax.numpy as jnp
from jax import lax
from jax.sharding import PartitionSpec as P

D = 8192
KV_HEADS = 8
PER_HEAD_CAP = 2


norm_epsilon = 1e-06


def swapped(value, axis, bit):
    return lax.ppermute(value, axis, [(i, i ^ 1 << bit) for i in range(lax.axis_size(axis))])


def cut_along(value, dim, peers):
    before, after = (value.shape[:dim], value.shape[dim + 1 :])
    return jnp.moveaxis(value.reshape(*before, peers, -1, *after), dim, 0)


def sent_and_summed(value, axis, dim):
    tiles = cut_along(value, dim, lax.axis_size(axis))
    arrived = lax.all_to_all(tiles, axis, split_axis=0, concat_axis=0, tiled=True)
    return arrived.astype(jnp.float32).sum(axis=0)


def side_by_side(arrays, axis, dim, along):
    ends, at = ([], 0)
    for a in arrays[:-1]:
        at += a.shape[along]
        ends.append(at)
    both = jnp.concatenate(arrays, axis=along)
    return tuple(jnp.split(lax.all_gather(both, axis, axis=dim, tiled=True), ends, axis=along))


def attend(queries, new_kv, kv_pool, counts, fill, order):
    slot_count, pool_pages, page_size, lane_width = kv_pool.shape
    head_dim = lane_width // 2
    requests = queries.shape[0]
    score_scale = 1.0 / head_dim**0.5
    position = jnp.arange(pool_pages, dtype=jnp.int32)
    position_in_order = jnp.sum(
        jnp.where(order[None, :] == position[:, None], position[None, :], 0), axis=1
    )
    count_ends = jnp.cumsum(counts)
    starts = count_ends - counts
    owner_index = jnp.sum(
        (count_ends[None, :] <= position_in_order[:, None]).astype(jnp.int32), axis=1
    )
    member = owner_index[:, None] == jnp.arange(requests, dtype=jnp.int32)[None, :]
    member_float = member.astype(jnp.float32)
    within = position_in_order - jnp.sum(jnp.where(member, starts[None, :], 0), axis=1)
    context = (counts - 1) * page_size + fill
    context_limit = jnp.sum(jnp.where(member, context[None, :], 0), axis=1)
    live_tokens = (
        within[:, None] * page_size + jnp.arange(page_size, dtype=jnp.int32)[None, :]
        < context_limit[:, None]
    )
    page_queries = jnp.einsum(
        "pr,rlgd->lpgd", member.astype(jnp.bfloat16), queries, preferred_element_type=jnp.float32
    ).astype(jnp.bfloat16)
    scores = (
        jnp.einsum(
            "lpgd,lptd->lpgt",
            page_queries,
            kv_pool[..., :head_dim],
            preferred_element_type=jnp.float32,
        )
        * score_scale
    )
    scores = jnp.where(live_tokens[None, :, None, :], scores, -1e30)
    page_top = jnp.max(scores, axis=3)
    fresh_score = (
        jnp.einsum(
            "rlgd,lrd->lrg", queries, new_kv[..., :head_dim], preferred_element_type=jnp.float32
        )
        * score_scale
    )
    masked_top = jnp.where(member.T[None, :, :, None], page_top[:, None, :, :], -1e30)
    request_top = jnp.maximum(fresh_score, jnp.max(masked_top, axis=2))
    page_ref = jnp.einsum("pr,lrg->lpg", member_float, request_top, precision=lax.Precision.HIGHEST)
    weight = jnp.where(live_tokens[None, :, None, :], jnp.exp(scores - page_ref[..., None]), 0.0)
    page_den = jnp.sum(weight, axis=3)
    page_num = jnp.einsum(
        "lpgt,lptd->lpgd",
        weight.astype(jnp.bfloat16),
        kv_pool[..., head_dim:],
        preferred_element_type=jnp.float32,
    )
    fresh_weight = jnp.exp(fresh_score - request_top)
    fresh_rounded = lax.optimization_barrier(fresh_weight.astype(jnp.bfloat16)).astype(jnp.float32)
    denominator = (
        jnp.einsum("pr,lpg->lrg", member_float, page_den, precision=lax.Precision.HIGHEST)
        + fresh_weight
    )
    numerator = jnp.einsum("pr,lpgd->lrgd", member_float, page_num, precision=lax.Precision.HIGHEST)
    numerator = numerator + fresh_rounded[..., None] * new_kv[:, :, None, head_dim:].astype(
        jnp.float32
    )
    attended = numerator / denominator[..., None]
    attended = jnp.transpose(attended, (1, 0, 2, 3)).astype(jnp.bfloat16)
    return attended.reshape(requests, -1)


def landing_table(destination, head_total, most_pages):
    sectioned_count = destination.shape[0]
    order_ids = jnp.arange(sectioned_count, dtype=jnp.int32)
    same_head = destination[:, None] == destination[None, :]
    earlier = order_ids[:, None] > order_ids[None, :]
    page_rank = jnp.sum((same_head & earlier).astype(jnp.int32), axis=1)
    matches = (
        destination[None, None, :] == jnp.arange(head_total, dtype=jnp.int32)[:, None, None]
    ) & (page_rank[None, None, :] == jnp.arange(most_pages, dtype=jnp.int32)[None, :, None])
    source_index = jnp.sum(jnp.where(matches, order_ids[None, None, :], 0), axis=2)
    source_valid = jnp.any(matches, axis=2)
    return (source_index, source_valid)


def per_device(
    queries,
    new_kv,
    kv_pool,
    page_counts,
    last_fill,
    page_order,
    hidden,
    out_weight,
    norm_gain,
    sectioned,
    routes,
):
    head_count = lax.axis_size("heads")
    slots_dev = new_kv.shape[0]
    head_dim = kv_pool.shape[3] // 2
    requests = hidden.shape[0]
    group_size = queries.shape[1] // (slots_dev * head_dim)
    page_data = sectioned[0, 0]
    source_index, source_valid = landing_table(routes[0, 0, :, 0], KV_HEADS, PER_HEAD_CAP)
    cache_total = head_count * slots_dev
    target = (
        (
            jnp.arange(head_count, dtype=jnp.int32)[None, :] * slots_dev
            + jnp.arange(slots_dev, dtype=jnp.int32)[:, None]
        )
        * KV_HEADS
        // cache_total
    )
    picked = source_index[target]
    present = source_valid[target]
    copies = cache_total // KV_HEADS
    piece_length = page_data.shape[1] // copies
    page_parts = page_data.reshape(page_data.shape[0], copies, piece_length, page_data.shape[2])
    part_of = (jnp.arange(head_count, dtype=jnp.int32) % copies)[None, :, None]
    outgoing = page_parts[picked, part_of]
    outgoing = jnp.where(present[..., None, None], outgoing, jnp.zeros_like(outgoing))
    landed = lax.all_to_all(outgoing, "heads", split_axis=1, concat_axis=1, tiled=True)
    head_position = lax.axis_index("heads")
    for bit_index in range(copies.bit_length() - 1):
        partner = swapped(landed, "heads", bit_index)
        upper_half = head_position // (1 << bit_index) % 2 == 1
        landed = jnp.where(
            upper_half,
            jnp.concatenate([partner, landed], axis=3),
            jnp.concatenate([landed, partner], axis=3),
        )
    arrival = landed[:, None]
    query_block = queries.reshape(requests, slots_dev, group_size, head_dim)
    attn = attend(query_block, new_kv, kv_pool, page_counts[0], last_fill[0], page_order[0])
    column_count = out_weight.shape[1] // head_count
    shared = sent_and_summed(
        lax.dot_general(
            out_weight, attn, (((0,), (1,)), ((), ())), preferred_element_type=jnp.float32
        ).astype(jnp.bfloat16),
        "heads",
        0,
    ).T
    column_start = lax.axis_index("heads") * column_count
    own_hidden = lax.dynamic_slice_in_dim(hidden, column_start, column_count, 1)
    own_gain = lax.dynamic_slice_in_dim(norm_gain, column_start, column_count, 0)
    mixed = own_hidden.astype(jnp.float32) + shared
    square_total = lax.psum(jnp.sum(mixed * mixed, axis=1), "heads")
    inverse_norm = lax.rsqrt(square_total / D + norm_epsilon)
    normed_shard = (mixed * inverse_norm[:, None] * own_gain.astype(jnp.float32)).astype(
        jnp.bfloat16
    )
    residual_shard = mixed.astype(jnp.bfloat16)
    residual_out, normed = side_by_side((residual_shard, normed_shard), "heads", 1, 0)
    return (residual_out, normed, arrival)


def solution(mesh):
    return jax.shard_map(
        per_device,
        mesh=mesh,
        in_specs=(
            P(("groups", "batch"), "heads"),
            P(("groups", "heads"), "batch", None),
            P(("groups", "heads"), "batch", None, None),
            P(("groups", "batch"), None),
            P(("groups", "batch"), None),
            P(("groups", "batch"), None),
            P(("groups", "batch"), None),
            P("heads", None),
            P(),
            P(("groups", "heads"), "batch", None, None, None),
            P(("groups", "heads"), "batch", None, None),
        ),
        out_specs=(
            P(("groups", "batch"), None),
            P(("groups", "batch"), None),
            P(("groups", "heads"), "batch", None, None, None, None),
        ),
        check_vma=False,
    )
```

profile of v0, /device:TPU:33, one launch (start us, length us, event | category | flops | bytes accessed | tf_op | source)
XLA Modules:
  0.0 238.0 jit_solution(8175433954071447057)
XLA Ops:
  0.7 0.7 iota_compare_fusion.6
  1.4 0.9 convert_reduce_fusion.2
  2.3 0.1 fusion.21
  2.5 0.2 and_reduce_fusion
  2.7 0.6 gather_fusion.1
  3.7 0.6 gather_fusion
  4.3 0.7 gather_fusion.2
  5.0 1.1 broadcast_select_fusion
  6.1 25.5 %all-to-all-start.1 = ((bf16[1,32,2,32,256]{4,3,2,0,1:T(8,128)(2,1)}), bf16[1,32,2,32,256]{4,3,2,0,1:T(8,128)(2,1)S(1)}, u32[]{:S(2)}, u32[]{:S(2)}) async-start(bf16[1,32,2,32,256]{4,3,2,0,1:T(8,128)(2,1)} %broadcast_select_fusion), calls=%async_computation.1 | async-start | bytes 2097152 | tf_op jit(solution)/shard_map/all_to_all | solution.py:158
  32.3 0.2 convolution_convert_fusion.1
  32.5 2.4 %fusion.48 = (f32[48,2]{1,0:T(8,128)S(1)}, f32[48,2,128]{2,1,0:T(2,128)S(1)}) fusion(bf16[1,48,128,256]{3,2,1,0:T(8,128)(2,1)} %param.13, bf16[48,2,128]{2,0,1:T(8,128)(2,1)S(1)} %convolution_convert_fusion.1, pred[48,128]{1,0:T(8,128)(4,1)S(1)} %add_compare_fusion), kind=kOutput, calls=%fused_computation.98 | convolution fusion | flops 3182496 | bytes 1653120 | tf_op jit(solution)/shard_map/lpgd,lptd->lpgt/dot_general | solution.py:65
  35.0 0.1 fusion.29
  35.6 0.2 fusion.46
  35.8 0.2 fusion.17
  36.0 2.0 fusion.1
  38.0 0.2 fusion.15
  38.2 2.8 %convolution_convert_fusion = bf16[16,8192]{1,0:T(8,128)(2,1)S(1)} fusion(bf16[256,8192]{1,0:T(8,128)(2,1)} %param.18, bf16[2,8,2,128]{3,2,1,0:T(2,128)(2,1)S(1)} %bitcast.135), kind=kOutput, calls=%fused_computation.3 | convolution fusion | flops 67239936 | bytes 4464640 | tf_op jit(solution)/shard_map/dot_general | solution.py:173
  41.0 0.7 copy.111
  41.7 45.4 %all-to-all-done.1 = bf16[1,32,2,32,256]{4,3,2,0,1:T(8,128)(2,1)S(1)} async-done(((bf16[1,32,2,32,256]{4,3,2,0,1:T(8,128)(2,1)}), bf16[1,32,2,32,256]{4,3,2,0,1:T(8,128)(2,1)S(1)}, u32[]{:S(2)}, u32[]{:S(2)}) %all-to-all-start.1) | async-done | bytes 1048608 | tf_op jit(solution)/shard_map/all_to_all | solution.py:158
  87.1 4.3 %all-to-all-start = ((bf16[32,256,16]{1,2,0:T(8,128)(2,1)}), bf16[32,256,16]{1,2,0:T(8,128)(2,1)S(1)}, u32[]{:S(2)}, u32[]{:S(2)}) async-start(bf16[32,256,16]{1,2,0:T(8,128)(2,1)} %bitcast.126), calls=%async_computation | async-start | bytes 524288 | tf_op jit(solution)/shard_map/all_to_all | solution.py:25
  91.4 1.1 collective-permute-start
  92.5 0.8 dynamic-slice_convert_fusion
  93.3 19.5 %all-to-all-done = bf16[32,256,16]{1,2,0:T(8,128)(2,1)S(1)} async-done(((bf16[32,256,16]{1,2,0:T(8,128)(2,1)}), bf16[32,256,16]{1,2,0:T(8,128)(2,1)S(1)}, u32[]{:S(2)}, u32[]{:S(2)}) %all-to-all-start) | async-done | bytes 262176 | tf_op jit(solution)/shard_map/all_to_all | solution.py:25
  112.9 0.8 fusion.36
  113.7 46.7 %psum.7 = f32[16]{0:T(128)S(1)} all-reduce(f32[16]{0:T(128)S(1)} %get-tuple-element.8), channel_id=1, replica_groups=mesh['groups'=2,'heads'=32,'batch'=4] {'heads'}, use_global_device_ids=true, to_apply=%region_10.11 | all-reduce | flops 16 | bytes 128 | tf_op jit(solution)/shard_map/psum | solution.py:183
  160.5 0.8 multiply_convert_fusion
  161.2 0.8 maximum_select_fusion.1
  162.0 0.1 collective-permute-start.1
  162.2 71.1 %all_gather.3 = bf16[32,8192]{1,0:T(8,128)(2,1)S(1)} all-gather(bf16[32,256]{1,0:T(8,128)(2,1)S(1)} %pad_maximum_fusion), channel_id=1, replica_groups=mesh['groups'=2,'heads'=32,'batch'=4] {'heads'}, dimensions={1}, use_global_device_ids=true | all-gather | bytes 540672 | tf_op jit(solution)/shard_map/all_gather | solution.py:35
  233.3 0.8 fusion.47
  234.1 0.8 fusion
  234.9 3.1 %maximum_select_fusion = bf16[1,1,32,2,128,256]{5,4,3,2,1,0:T(8,128)(2,1)} fusion(bf16[1,1,32,2,64,256]{5,4,3,2,1,0:T(8,128)(2,1)S(1)} %fusion, bf16[1,1,32,2,64,256]{5,4,3,2,1,0:T(8,128)(2,1)S(1)} %bitcast.133, pred[]{:T(512)S(6)} %eq.109), kind=kLoop, calls=%fused_computation.4 | loop fusion | flops 18874368 | bytes 8388609 | tf_op jit(solution)/shard_map/jit(_where)/select_n | solution.py:163
  (50 shorter events, 1.7 us)
Async XLA Ops:
  0.6 3.7 %copy-start = (bf16[1,1,8,128,256]{4,3,2,1,0:T(8,128)(2,1)S(1)}, bf16[1,1,8,128,256]{4,3,2,1,0:T(8,128)(2,1)}, u32[]{:S(2)}) copy-start(bf16[1,1,8,128,256]{4,3,2,1,0:T(8,128)(2,1)} %param.20) | copy-start | bytes 1572868
  0.6 31.0 %copy-start.3 = (s32[1,16]{1,0:T(1,128)S(1)}, s32[1,16]{1,0:T(1,128)}, u32[]{:S(2)}) copy-start(s32[1,16]{1,0:T(1,128)} %param.14) | copy-start | bytes 196
  0.7 31.2 %copy-start.1 = (bf16[16,256]{1,0:T(8,128)(2,1)S(1)}, bf16[16,256]{1,0:T(8,128)(2,1)}, u32[]{:S(2)}) copy-start(bf16[16,256]{1,0:T(8,128)(2,1)} %param.11) | copy-start | bytes 24580
  0.7 31.2 %copy-start.5 = (s32[1,48]{1,0:T(1,128)S(1)}, s32[1,48]{1,0:T(1,128)}, u32[]{:S(2)}) copy-start(s32[1,48]{1,0:T(1,128)} %param.16) | copy-start | bytes 580
  0.7 31.4 %copy-start.4 = (s32[1,16]{1,0:T(1,128)S(1)}, s32[1,16]{1,0:T(1,128)}, u32[]{:S(2)}) copy-start(s32[1,16]{1,0:T(1,128)} %param.15) | copy-start | bytes 196
  3.3 31.7 %copy-start.2 = (bf16[1,16,256]{2,1,0:T(8,128)(2,1)S(1)}, bf16[1,16,256]{2,1,0:T(8,128)(2,1)}, u32[]{:S(2)}) copy-start(bf16[1,16,256]{2,1,0:T(8,128)(2,1)} %param.12) | copy-start | bytes 24580
  6.1 81.0 %all-to-all-start.1 = ((bf16[1,32,2,32,256]{4,3,2,0,1:T(8,128)(2,1)}), bf16[1,32,2,32,256]{4,3,2,0,1:T(8,128)(2,1)S(1)}, u32[]{:S(2)}, u32[]{:S(2)}) async-start(bf16[1,32,2,32,256]{4,3,2,0,1:T(8,128)(2,1)} %broadcast_select_fusion), calls=%async_computation.1 | async-start | bytes 2097152 | tf_op jit(solution)/shard_map/all_to_all | solution.py:158
  87.1 25.7 %all-to-all-start = ((bf16[32,256,16]{1,2,0:T(8,128)(2,1)}), bf16[32,256,16]{1,2,0:T(8,128)(2,1)S(1)}, u32[]{:S(2)}, u32[]{:S(2)}) async-start(bf16[32,256,16]{1,2,0:T(8,128)(2,1)} %bitcast.126), calls=%async_computation | async-start | bytes 524288 | tf_op jit(solution)/shard_map/all_to_all | solution.py:25
  91.4 69.8 %collective-permute-start = (bf16[1,32,2,32,256]{4,3,2,1,0:T(8,128)(2,1)S(1)}, bf16[1,32,2,32,256]{4,3,2,1,0:T(8,128)(2,1)S(1)}, u32[]{:S(2)}, u32[]{:S(2)}) collective-permute-start(bf16[1,32,2,32,256]{4,3,2,1,0:T(8,128)(2,1)S(1)} %bitcast.128), channel_id=1, source_target_pairs={{0,4},{4,0},{8,12},{12,8},{16,20},{20,16},{24,28},{28,24},{32,36},... | collective-permute-start | bytes 3145736 | tf_op jit(solution)/shard_map/ppermute | solution.py:15
  162.0 72.8 %collective-permute-start.1 = (bf16[1,32,2,64,256]{4,3,2,1,0:T(8,128)(2,1)S(1)}, bf16[1,32,2,64,256]{4,3,2,1,0:T(8,128)(2,1)S(1)}, u32[]{:S(2)}, u32[]{:S(2)}) collective-permute-start(bf16[1,32,2,64,256]{4,3,2,1,0:T(8,128)(2,1)S(1)} %maximum_select_fusion.1), channel_id=1, source_target_pairs={{0,8},{4,12},{8,0},{12,4},{16,24},{20,28},{24,16},{28,20},{32,40},... | collective-permute-start | bytes 6291464 | tf_op jit(solution)/shard_map/ppermute | solution.py:15
where the time goes:
time: 238 us
  blocking collectives  118 us (50%)
  waiting for transfers between devices  64.9 us (27%)
  starting transfers between devices  31 us (13%)
  other arithmetic  11 us (5%)
  matrix products  8.04 us (3%)
  local copies, waits for them, and re-layouts  4.27 us (2%)
    all_gather x1, blocking collectives, side_by_side(): lax.all_gather(both, axis, axis=dim, tiled=True)  71.1 us
    psum x1, blocking collectives, per_device(): square_total = lax.psum(jnp.sum(mixed * mixed, axis=1), 'heads')  46.7 us
    all_to_all x1, waiting for transfers between devices, per_device(): lax.all_to_all(outgoing, 'heads', split_axis=1, concat_axis=1, tiled=True)  45.4 us
    all_to_all x1, starting transfers between devices, per_device(): lax.all_to_all(outgoing, 'heads', split_axis=1, concat_axis=1, tiled=True)  25.5 us
    all_to_all x1, waiting for transfers between devices, sent_and_summed(): lax.all_to_all(tiles, axis, split_axis=0, concat_axis=0, tiled=True)  19.5 us
  transfers between devices with their start and end apart: 4, of which 2 were waited for; matrix products, arithmetic and copies ran while one was open for 6% of the time, Pallas kernels for 0%

commit v1 on v0

v1 whole, which is shorter than its diff:
```python
import functools

import jax
import jax.numpy as jnp
from jax import lax
from jax.experimental import pallas as pl
from jax.experimental.pallas import tpu as pltpu
from jax.sharding import PartitionSpec as P

KV_HEADS = 8
PER_HEAD_CAP = 2
CORES = 2
CHUNK_PAGES = 8
norm_epsilon = 1e-06

MESH = pl.DeviceIdType.MESH
F32 = jnp.float32
BF16 = jnp.bfloat16


def page_limits(counts_ref, fill_ref, order_ref, page_size):
    requests, pool = counts_ref.shape[1], order_ref.shape[1]
    lane = lax.broadcasted_iota(jnp.int32, (requests, requests), 1)
    row = lax.broadcasted_iota(jnp.int32, (requests, requests), 0)
    counts = jnp.broadcast_to(counts_ref[...].astype(F32), (requests, requests))
    fill = jnp.broadcast_to(fill_ref[...].astype(F32), (requests, requests))
    count_col = jnp.sum(jnp.where(lane == row, counts, 0.0), axis=1, keepdims=True)
    fill_col = jnp.sum(jnp.where(lane == row, fill, 0.0), axis=1, keepdims=True)
    ends = jnp.sum(jnp.where(lane <= row, counts, 0.0), axis=1, keepdims=True)
    starts = ends - count_col
    context = (count_col - 1.0) * page_size + fill_col
    place = lax.broadcasted_iota(jnp.int32, (requests, 128), 1).astype(F32)
    live = jnp.clip(context - page_size * (place - starts), 0.0, float(page_size))
    live = jnp.where((place >= starts) & (place < ends), live, 0.0)
    order = jnp.broadcast_to(order_ref[...], (pool, pool))
    lane = lax.broadcasted_iota(jnp.int32, (pool, pool), 1)
    row = lax.broadcasted_iota(jnp.int32, (pool, pool), 0)
    order_col = jnp.sum(jnp.where(lane == row, order.astype(F32), 0.0), axis=1, keepdims=True)
    page = lax.broadcasted_iota(jnp.int32, (pool, 128), 1).astype(F32)
    one_hot = jnp.where(order_col == page, 1.0, 0.0).astype(BF16)
    return jnp.dot(live[:, :pool].astype(BF16), one_hot, preferred_element_type=F32)


def attend(q_ref, new_ref, kv, scores, limits):
    pool, page_size, width = kv.shape
    head_dim = width // 2
    requests = q_ref.shape[0]
    groups = q_ref.shape[1] // head_dim
    scale = 1.0 / head_dim**0.5
    q = jnp.concatenate([q_ref[:, g * head_dim : (g + 1) * head_dim] for g in range(groups)], axis=0)
    limits = jnp.concatenate([limits] * groups, axis=0)
    rows = groups * requests
    new_key = new_ref[:, :head_dim].astype(F32)
    new_value = new_ref[:, head_dim:].astype(F32)
    new_key = jnp.concatenate([new_key] * groups, axis=0)
    new_value = jnp.concatenate([new_value] * groups, axis=0)
    fresh = jnp.sum(q.astype(F32) * new_key, axis=1, keepdims=True) * scale
    token = lax.broadcasted_iota(jnp.int32, (rows, page_size), 1).astype(F32)
    top = jnp.full((rows, page_size), -1e30, F32)
    for first in range(0, pool, CHUNK_PAGES):
        keys = kv[first : first + CHUNK_PAGES, :, :head_dim].reshape(CHUNK_PAGES * page_size, head_dim)
        s = lax.dot_general(q, keys, (((1,), (1,)), ((), ())), preferred_element_type=F32) * scale
        for i in range(CHUNK_PAGES):
            part = s[:, i * page_size : (i + 1) * page_size]
            part = jnp.where(token < limits[:, first + i : first + i + 1], part, -1e30)
            top = jnp.maximum(top, part)
            scores[:, (first + i) * page_size : (first + i + 1) * page_size] = part
    top = jnp.maximum(jnp.max(top, axis=1, keepdims=True), fresh)
    den = jnp.zeros((rows, page_size), F32)
    num = jnp.zeros((rows, head_dim), F32)
    for first in range(0, pool, CHUNK_PAGES):
        cols = slice(first * page_size, (first + CHUNK_PAGES) * page_size)
        w = jnp.exp(scores[:, cols] - top)
        for i in range(CHUNK_PAGES):
            den = den + w[:, i * page_size : (i + 1) * page_size]
        values = kv[first : first + CHUNK_PAGES, :, head_dim:].reshape(CHUNK_PAGES * page_size, head_dim)
        num = num + jnp.dot(w.astype(BF16), values, preferred_element_type=F32)
    fresh_w = jnp.exp(fresh - top)
    den = jnp.sum(den, axis=1, keepdims=True) + fresh_w
    num = num + fresh_w.astype(BF16).astype(F32) * new_value
    out = (num / den).astype(BF16)
    return jnp.concatenate([out[g * requests : (g + 1) * requests] for g in range(groups)], axis=1)


def pack_slots(routes, pages, slots):
    count = pages.shape[0]
    heads, cap = slots.shape[:2]
    dest = [routes[j] for j in range(count)]
    rank = []
    for j in range(count):
        r = jnp.int32(0)
        for i in range(j):
            r = r + (dest[i] == dest[j]).astype(jnp.int32)
        rank.append(r)
    key = [dest[j] * cap + rank[j] for j in range(count)]
    for h in range(heads):
        for k in range(cap):
            index, found = jnp.int32(0), jnp.int32(0)
            for j in range(count):
                hit = (key[j] == h * cap + k).astype(jnp.int32)
                index = index + hit * j
                found = found + hit
            page = pages[index]
            slots[h, k] = jnp.where(found > 0, page, jnp.zeros_like(page))


def kernel(
    chips,
    q_ref,
    new_ref,
    counts_ref,
    fill_ref,
    order_ref,
    gain_ref,
    routes_ref,
    kv_in,
    hidden_in,
    weight_in,
    pages_in,
    arr,
    residual_ref,
    normed_ref,
    kv,
    weight,
    hidden,
    pages,
    slots,
    scores,
    part,
    sibling_part,
    terms,
    got_terms,
    blocks,
    load_sem,
    own_sem,
    page_send,
    near_sem,
    far_send,
    far_sem,
    partner_sem,
    core_send,
    core_sem,
    part_send,
    part_sem,
    term_send,
    term_sem,
    block_send,
    block_sem,
    share_send,
    share_sem,
):
    pairs = chips // 2
    reach = pairs // 2
    block = blocks.shape[3]
    a = lax.axis_index("heads")
    z, c = a // CORES, a % CORES
    pair, parity = z // 2, z % 2
    partner_z = z + 1 - 2 * parity
    sibling = z * CORES + (1 - c)

    def lane(zt):
        return zt * CORES + c

    def remote(src, dst, send, recv, dev):
        return pltpu.make_async_remote_copy(
            src_ref=src, dst_ref=dst, send_sem=send, recv_sem=recv, device_id={"heads": dev}, device_id_type=MESH
        )

    barrier = pltpu.get_barrier_semaphore()
    pl.semaphore_signal(barrier, inc=1, device_id={"heads": sibling}, device_id_type=MESH)
    for i in range(1, chips):
        pl.semaphore_signal(barrier, inc=1, device_id={"heads": lane((z + i) % chips)}, device_id_type=MESH)

    own_column = pl.multiple_of((c * chips + z) * block, block)
    loads = [
        pltpu.make_async_copy(pages_in, pages, load_sem.at[0]),
        pltpu.make_async_copy(kv_in, kv, load_sem.at[1]),
        pltpu.make_async_copy(weight_in, weight, load_sem.at[2]),
        pltpu.make_async_copy(hidden_in.at[:, pl.ds(own_column, block)], hidden, load_sem.at[3]),
    ]
    for copy in loads:
        copy.start()
    loads[0].wait()
    pack_slots(routes_ref, pages, slots)
    pl.semaphore_wait(barrier, chips)

    started = []

    def go(copy):
        copy.start()
        started.append(copy)

    own = pltpu.make_async_copy(slots.at[pair], arr.at[a], own_sem)
    own.start()
    go(remote(slots.at[pair], arr.at[a], page_send.at[0], partner_sem, lane(partner_z)))

    def clockwise(k):
        h = (pair + k) % pairs
        go(remote(slots.at[h], arr.at[a], page_send.at[2 * k - 1], near_sem.at[(k - 1) * 2 + parity], lane(2 * h)))

    def counter(k):
        h = (pair + pairs - k) % pairs
        go(remote(slots.at[h], arr.at[a], page_send.at[2 * k], near_sem.at[(k - 1) * 2 + parity], lane(2 * h + 1)))

    def opposite():
        h = (pair + reach) % pairs
        go(
            remote(
                slots.at[h],
                arr.at[a],
                page_send.at[2 * reach - 1],
                near_sem.at[2 * (reach - 1)],
                lane(2 * h + 1 - parity),
            )
        )

    def source(m, side):
        if m == 2 * (reach - 1):
            zs = 2 * ((pair + reach) % pairs) + 1 - side
        else:
            k, sp = m // 2 + 1, m % 2
            zs = 2 * ((pair + pairs + (2 * side - 1) * k) % pairs) + sp
        return zs

    def to_sibling(zs):
        row = arr.at[lane(zs)]
        go(remote(row, row, core_send.at[zs], core_sem.at[zs], sibling))

    def relay_near(m):
        zs = source(m, parity)
        row = arr.at[lane(zs)]
        remote(row, row, far_send.at[m], near_sem.at[m], lane(partner_z)).wait_recv()
        go(remote(row, row, far_send.at[m], far_sem.at[m], lane(partner_z)))
        to_sibling(zs)

    def take_far(m):
        zs = source(m, 1 - parity)
        row = arr.at[lane(zs)]
        remote(row, row, far_send.at[m], far_sem.at[m], lane(partner_z)).wait_recv()
        to_sibling(zs)

    clockwise(1)
    counter(1)
    clockwise(2)
    counter(2)

    limits = page_limits(counts_ref, fill_ref, order_ref, kv.shape[1])
    loads[1].wait()
    attn = attend(q_ref, new_ref, kv, scores, limits)
    loads[2].wait()
    for half in range(CORES):

        def project(zz, _, half=half):
            columns = pl.ds(pl.multiple_of((half * chips + zz) * block, block), block)
            part[half, zz] = jnp.dot(attn, weight[:, columns], preferred_element_type=F32)
            return 0

        lax.fori_loop(0, chips, project, 0, unroll=4)

    own.wait()
    to_sibling(z)
    exchange = remote(part.at[1 - c], sibling_part, part_send, part_sem, sibling)
    exchange.start()
    exchange.wait_recv()

    def add_cores(zz, _):
        terms[zz] = (part[c, zz] + sibling_part[zz]).astype(BF16)
        return 0

    lax.fori_loop(0, chips, add_cores, 0, unroll=4)
    total = part[c, z] + sibling_part[z]
    for i in range(1, chips):
        zt = (z + i) % chips
        go(remote(terms.at[zt], got_terms.at[i - 1], term_send.at[i - 1], term_sem.at[i - 1], lane(zt)))
    clockwise(3)
    counter(3)
    relay_near(0)
    relay_near(1)
    remote(arr.at[lane(partner_z)], arr.at[lane(partner_z)], page_send.at[0], partner_sem, sibling).wait_recv()
    to_sibling(partner_z)

    for i in range(1, chips):
        remote(terms.at[0], got_terms.at[i - 1], term_send.at[i - 1], term_sem.at[i - 1], sibling).wait_recv()
        total = total + got_terms[i - 1].astype(F32)
    loads[3].wait()
    blocks[c, z] = (hidden[...].astype(F32) + total).astype(BF16)
    relay_near(2)
    relay_near(3)
    mine = blocks.at[c, z]
    for i in range(1, chips):
        go(remote(mine, mine, block_send.at[i - 1], block_sem.at[i - 1], lane((z + i) % chips)))
    opposite()
    take_far(0)
    take_far(1)
    take_far(2)
    take_far(3)
    for i in range(1, chips):
        theirs = blocks.at[c, (z + chips - i) % chips]
        remote(theirs, theirs, block_send.at[i - 1], block_sem.at[i - 1], sibling).wait_recv()
    share = remote(blocks.at[c], blocks.at[c], share_send, share_sem, sibling)
    share.start()
    relay_near(4)
    relay_near(5)
    remote(blocks.at[1 - c], blocks.at[1 - c], share_send, share_sem, sibling).wait_recv()

    def squares(b, acc):
        x = blocks[b // chips, b % chips].astype(F32)
        return acc + x * x

    width = CORES * chips * block
    acc = lax.fori_loop(0, CORES * chips, squares, jnp.zeros(blocks.shape[2:], F32), unroll=4)
    inverse = lax.rsqrt(jnp.sum(acc, axis=1, keepdims=True) / width + norm_epsilon)

    def finish(b, _):
        columns = pl.ds(pl.multiple_of(b * block, block), block)
        x = blocks[b // chips, b % chips]
        residual_ref[:, columns] = x
        normed_ref[:, columns] = (x.astype(F32) * inverse * gain_ref[:, columns].astype(F32)).astype(BF16)
        return 0

    lax.fori_loop(0, CORES * chips, finish, 0, unroll=4)

    relay_near(6)
    take_far(4)
    take_far(5)
    take_far(6)
    for i in range(chips):
        theirs = arr.at[i * CORES + 1 - c]
        remote(theirs, theirs, core_send.at[i], core_sem.at[i], sibling).wait_recv()
    exchange.wait_send()
    share.wait_send()
    for copy in started:
        copy.wait_send()


def per_device(
    queries,
    new_kv,
    kv_pool,
    page_counts,
    last_fill,
    page_order,
    hidden,
    out_weight,
    norm_gain,
    sectioned,
    routes,
):
    head_count = lax.axis_size("heads")
    chips = head_count // CORES
    requests, width = hidden.shape
    _, pool, page_size, kv_width = kv_pool.shape
    page_count = sectioned.shape[2]
    block = width // head_count
    pairs = chips // 2
    near = pairs - 1
    if pairs != KV_HEADS or new_kv.shape[0] != 1:
        raise ValueError("unexpected layout")
    vmem = pl.BlockSpec(memory_space=pltpu.VMEM)
    smem = pl.BlockSpec(memory_space=pltpu.SMEM)
    anywhere = pl.BlockSpec(memory_space=pl.ANY)
    dma = pltpu.SemaphoreType.DMA
    slot_shape = (PER_HEAD_CAP, page_size, kv_width)
    arrival, residual, normed = pl.pallas_call(
        functools.partial(kernel, chips),
        out_shape=(
            jax.ShapeDtypeStruct((head_count, *slot_shape), BF16),
            jax.ShapeDtypeStruct((requests, width), BF16),
            jax.ShapeDtypeStruct((requests, width), BF16),
        ),
        in_specs=[vmem] * 6 + [smem] + [anywhere] * 4,
        out_specs=(anywhere, vmem, vmem),
        scratch_shapes=[
            pltpu.VMEM((pool, page_size, kv_width), BF16),
            pltpu.VMEM(out_weight.shape, BF16),
            pltpu.VMEM((requests, block), BF16),
            pltpu.VMEM((page_count, page_size, kv_width), BF16),
            pltpu.VMEM((KV_HEADS, *slot_shape), BF16),
            pltpu.VMEM((requests * queries.shape[1] * 2 // kv_width, pool * page_size), F32),
            pltpu.VMEM((CORES, chips, requests, block), F32),
            pltpu.VMEM((chips, requests, block), F32),
            pltpu.VMEM((chips, requests, block), BF16),
            pltpu.VMEM((chips - 1, requests, block), BF16),
            pltpu.VMEM((CORES, chips, requests, block), BF16),
            dma((4,)),
            dma,
            dma((pairs,)),
            dma((near,)),
            dma((near,)),
            dma((near,)),
            dma,
            dma((chips,)),
            dma((chips,)),
            dma,
            dma,
            dma((chips - 1,)),
            dma((chips - 1,)),
            dma((chips - 1,)),
            dma((chips - 1,)),
            dma,
            dma,
        ],
        compiler_params=pltpu.CompilerParams(
            collective_id=0, has_side_effects=True, vmem_limit_bytes=40 * 1024 * 1024
        ),
    )(
        queries,
        new_kv[0],
        page_counts,
        last_fill,
        page_order,
        norm_gain.reshape(1, width),
        routes.reshape(page_count),
        kv_pool[0],
        hidden,
        out_weight,
        sectioned[0, 0],
    )
    return (residual, normed, arrival[None, None])


def solution(mesh):
    return jax.shard_map(
        per_device,
        mesh=mesh,
        in_specs=(
            P(("groups", "batch"), "heads"),
            P(("groups", "heads"), "batch", None),
            P(("groups", "heads"), "batch", None, None),
            P(("groups", "batch"), None),
            P(("groups", "batch"), None),
            P(("groups", "batch"), None),
            P(("groups", "batch"), None),
            P("heads", None),
            P(),
            P(("groups", "heads"), "batch", None, None, None),
            P(("groups", "heads"), "batch", None, None),
        ),
        out_specs=(
            P(("groups", "batch"), None),
            P(("groups", "batch"), None),
            P(("groups", "heads"), "batch", None, None, None, None),
        ),
        check_vma=False,
    )
```

time: 238 us -> 117 us (0.49)
  blocking collectives: 118 us -> 0 us
  Pallas kernels: 0 us -> 101 us
  waiting for transfers between devices: 64.9 us -> 0 us
  starting transfers between devices: 31 us -> 0 us
  other arithmetic: 11 us -> 0 us
  local copies, waits for them, and re-layouts: 4.27 us -> 14.2 us
  matrix products: 8.04 us -> 0 us
    pallas_call x0 -> x1, Pallas kernels: none -> 101 us  [per_device(): pl.pallas_call(functools.partial(kernel, chips), out_shape=(jax.ShapeDtyp...]
    all_gather x1 -> x0, blocking collectives: 71.1 us -> none  [side_by_side(): lax.all_gather(both, axis, axis=dim, tiled=True)]
    all_to_all x2 -> x0, waiting for transfers between devices: 64.9 us -> none  [the longest x1 45.4 us: per_device(): lax.all_to_all(outgoing, 'heads', split_axis=1, concat_axis=1, tiled=True)]
    psum x1 -> x0, blocking collectives: 46.7 us -> none  [per_device(): square_total = lax.psum(jnp.sum(mixed * mixed, axis=1), 'heads')]
    all_to_all x2 -> x0, starting transfers between devices: 29.7 us -> none  [the longest x1 25.5 us: per_device(): lax.all_to_all(outgoing, 'heads', split_axis=1, concat_axis=1, tiled=True)]
    unnamed x12 -> x23, local copies, waits for them, and re-layouts: 0.03 us -> 13.5 us
    dot_general x8 -> x0, matrix products: 8.04 us -> none  [the longest x1 2.84 us: per_device(): lax.dot_general(out_weight, attn, (((0,), (1,)), ((), ())), preferred_ele...]
    select_n x6 -> x0, other arithmetic: 5 us -> none  [the longest x2 3.86 us: per_device(): jnp.where(upper_half, jnp.concatenate([partner, landed], axis=3), jnp.con...]
  transfers between devices with their start and end apart: 4 -> 0, of which waited for: 2 -> 0; matrix products, arithmetic and copies ran while one was open for 6% -> 0% of each run, Pallas kernels for 0% -> 0%
where the time goes in v1:
time: 117 us; the launch traced here: 116 us
  Pallas kernels  101 us (86%)
  local copies, waits for them, and re-layouts  14.2 us (12%)
    pallas_call x1, Pallas kernels, per_device(): pl.pallas_call(functools.partial(kernel, chips), out_shape=(jax.ShapeDtyp...  101 us
    unnamed x23, local copies, waits for them, and re-layouts  13.5 us

profile of v1, /device:TPU:33, one launch (start us, length us, event | category | flops | bytes accessed | tf_op | source)
XLA Modules:
  0.0 116.2 jit_solution(1054986815616304207)
XLA Ops:
  0.6 0.7 reshape.12.gain_ref
  1.4 0.0 copy-start
  1.4 2.2 %copy-done = bf16[256,8192]{1,0:T(8,128)(2,1)S(1)} copy-done((bf16[256,8192]{1,0:T(8,128)(2,1)S(1)}, bf16[256,8192]{1,0:T(8,128)(2,1)}, u32[]{:S(2)}) %copy-start) | copy-done | bytes 4194328
  3.6 0.0 copy-start.1
  3.6 1.9 %copy-done.1 = bf16[1,48,128,256]{3,2,1,0:T(8,128)(2,1)S(1)} copy-done((bf16[1,48,128,256]{3,2,1,0:T(8,128)(2,1)S(1)}, bf16[1,48,128,256]{3,2,1,0:T(8,128)(2,1)}, u32[]{:S(2)}) %copy-start.1) | copy-done | bytes 3145752
  5.5 0.0 copy-start.2
  5.5 1.0 copy-done.2
  6.5 0.0 copy-start.3
  6.5 0.9 copy-done.3
  7.4 0.0 copy-start.4
  7.4 0.7 copy-done.4
  8.1 0.0 copy-start.5
  8.1 0.7 copy-done.5
  8.8 0.0 copy-start.6
  8.8 0.7 copy-done.6
  9.5 0.0 copy-start.7
  9.5 0.7 copy-done.7
  10.2 0.0 copy-start.8
  10.2 0.7 copy-done.8
  10.8 0.0 copy-start.9
  10.8 0.7 copy-done.9
  11.5 101.3 %shard_map.130 = (bf16[32,2,128,256]{3,2,1,0:T(8,128)(2,1)S(1)}, bf16[16,8192]{1,0:T(8,128)(2,1)S(1)}, bf16[16,8192]{1,0:T(8,128)(2,1)S(1)}) custom-call(bf16[16,256]{1,0:T(8,128)(2,1)S(1)} %copy-done.4, bf16[16,256]{1,0:T(8,128)(2,1)S(1)} %bitcast.8, s32[1,16]{1,0:T(1,128)S(1)} %copy-done.6, s32[1,16]{1,0:T(1,128)S(1)} %copy-done.7, s32[1,48]{1,0:T(1,128)S(1)} %copy-done.8, ...), custom_call_target="tpu_custom_call" | custom-call | tf_op jit(solution)/shard_map/pallas_call | solution.py:364
  112.8 0.7 copy.17
  113.5 0.7 copy.18
  114.2 2.0 %copy.19 = bf16[1,1,32,2,128,256]{5,4,3,2,1,0:T(8,128)(2,1)} copy(bf16[1,1,32,2,128,256]{5,4,3,2,1,0:T(8,128)(2,1)S(1)} %bitcast.5) | data formatting | bytes 8388608
Async XLA Ops:
  1.4 2.2 %copy-start = (bf16[256,8192]{1,0:T(8,128)(2,1)S(1)}, bf16[256,8192]{1,0:T(8,128)(2,1)}, u32[]{:S(2)}) copy-start(bf16[256,8192]{1,0:T(8,128)(2,1)} %weight_in.1) | copy-start | bytes 12582916
  3.6 1.9 %copy-start.1 = (bf16[1,48,128,256]{3,2,1,0:T(8,128)(2,1)S(1)}, bf16[1,48,128,256]{3,2,1,0:T(8,128)(2,1)}, u32[]{:S(2)}) copy-start(bf16[1,48,128,256]{3,2,1,0:T(8,128)(2,1)} %param.13) | copy-start | bytes 9437188
  5.5 1.0 copy-start.2
  6.5 0.9 copy-start.3
  7.4 0.7 copy-start.4
  8.1 0.7 copy-start.5
  8.8 0.7 copy-start.6
  9.5 0.7 copy-start.7
  10.2 0.7 copy-start.8
  10.8 0.7 copy-start.9
